TPU v7x, 8 devices: a whole 2x2x1 slice. The times are simulated.
8 devices in a mesh: dp: 2 (over y, z), tp: 4 (over x, core).
Axes of the slice: x: 2, y: 2, z: 1, core: 2. Of those that a mesh axis runs over, the one named last changes fastest.
Arguments:
- x: bfloat16 [2816, 3072], P(('dp', 'tp')), parts along dimension 0
- dy: bfloat16 [2816, 3072], P(('dp', 'tp')), parts along dimension 0
- gate: bfloat16 [2816, 8192], P('dp', 'tp'), parts along dimension 0
- up: bfloat16 [2816, 8192], P('dp', 'tp'), parts along dimension 0
- w_gate: bfloat16 [3072, 8192], P(None, 'tp')
- w_up: bfloat16 [3072, 8192], P(None, 'tp')
- w_down: bfloat16 [8192, 3072], P('tp')
Outputs:
- output 1: bfloat16 [2816, 3072], P(('dp', 'tp')), parts along dimension 0
- output 2: bfloat16 [6144, 8192], P('dp', 'tp'), parts along dimension 0
- output 3: bfloat16 [6144, 8192], P('dp', 'tp'), parts along dimension 0
- output 4: bfloat16 [16384, 3072], P(('dp', 'tp')), parts along dimension 0
There are 2 independent parts. A program takes and returns all parts, laid end to end along the dimension named above; an argument that names none is the same for every part.
All inputs are finite; a program needn't handle non-finite values.
Results may differ from a plain program's by a relative error of at most 0.012.
Values are sent between devices in bfloat16 or wider.
A program may use at most 2 GiB of HBM per device.

v0:
```python
import jax
import jax.numpy as jnp


def act(gate, up):
    return jax.nn.silu(gate) * up


def solution(mesh):
    def step(x, dy, gate, up, w_gate, w_up, w_down):
        hidden, back = jax.vjp(act, gate.astype(jnp.float32), up.astype(jnp.float32))
        d_hidden = jnp.dot(dy, w_down.T, preferred_element_type=jnp.float32)
        d_gate, d_up = (g.astype(jnp.bfloat16) for g in back(d_hidden))
        dx = jnp.dot(d_gate, w_gate.T) + jnp.dot(d_up, w_up.T)
        groups = mesh.shape["dp"]

        def by_group(a, b):
            a, b = (t.reshape(groups, -1, t.shape[-1]) for t in (a, b))
            product = jnp.einsum("gta,gtb->gab", a, b, preferred_element_type=jnp.float32)
            return product.astype(jnp.bfloat16).reshape(-1, b.shape[-1])

        return dx, by_group(x, d_gate), by_group(x, d_up), by_group(hidden.astype(jnp.bfloat16), dy)

    return step
```

profile of v0, /device:TPU:0, one launch (start us, length us, event | category | flops | bytes accessed | tf_op | source)
XLA Modules:
  0.0 288.8 jit_solution(16339886866546792146)
XLA Ops:
  7.2 0.0 all-gather.11.cloned.1.call-start
  7.2 0.7 all-gather.11.cloned.1.call-update
  7.9 0.0 all-gather.13.cloned.1.call-start
  7.9 0.7 all-gather.13.cloned.1.call-update
  8.6 0.0 reduce-scatter.4.cloned.1.call-start
  8.7 60.9 %all-gather.11.cloned.1.call-done = bf16[1408,3072]{1,0:T(8,128)(2,1)} async-done(((bf16[352,3072]{1,0:T(8,128)(2,1)}), bf16[1408,3072]{1,0:T(8,128)(2,1)}) %all-gather.11.cloned.1.call-update) | async-done | bytes 8650768 | tf_op args[1]
  69.6 30.2 %fusion.6 = (bf16[1408,2048]{1,0:T(8,128)(2,1)S(1)}, f32[1408,2048]{1,0:T(8,128)}) fusion(bf16[1408,2048]{1,0:T(8,128)(2,1)} %param.3, bf16[1408,2048]{1,0:T(8,128)(2,1)} %param.2, bf16[1408,3072]{1,0:T(8,128)(2,1)} %all-gather.11.cloned.1.call-done, bf16[2048,3072]{1,0:T(8,128)(2,1)} %param.1), kind=kOutput, calls=%fused_computation.14 | convolution fusion | flops 17754226688 | bytes 50069504 | tf_op jit(solution)/dot_general | solution.py:12
  99.8 0.0 copy-start
  99.8 24.3 %fusion.9 = bf16[1408,3072]{1,0:T(8,128)(2,1)} fusion(bf16[1408,2048]{1,0:T(8,128)(2,1)S(1)} %get-tuple-element.4, bf16[3072,2048]{1,0:T(8,128)(2,1)} %param.4), kind=kOutput, calls=%fused_computation.19 | convolution fusion | flops 17716740096 | bytes 27000832 | tf_op jit(solution)/dot_general | solution.py:14
  124.1 0.0 copy-done
  124.1 30.9 %convolution_add_fusion = bf16[1408,3072]{1,0:T(8,128)(2,1)} fusion(bf16[1408,3072]{1,0:T(8,128)(2,1)} %fusion.9, bf16[3072,2048]{1,0:T(8,128)(2,1)} %param.5, f32[1408,2048]{1,0:T(8,128)} %get-tuple-element.5, bf16[1408,2048]{1,0:T(8,128)(2,1)} %param.3), kind=kOutput, calls=%fused_computation.17 | convolution fusion | flops 17741250560 | bytes 47185920 | tf_op jit(solution)/dot_general | solution.py:14
  155.1 0.0 reduce-scatter.4.cloned.1.call-update
  155.1 0.0 all-gather.13.cloned.1.call-done
  155.1 25.9 %convert_bitcast_fusion.1 = bf16[3072,2048]{0,1:T(8,128)(2,1)} fusion(bf16[1408,2048]{1,0:T(8,128)(2,1)} %copy-done, bf16[1408,3072]{1,0:T(8,128)(2,1)} %all-gather.13.cloned.1.call-done), kind=kOutput, calls=%fused_computation.7 | convolution fusion | flops 17723031552 | bytes 27000832 | tf_op jit(solution)/gta,gtb->gab/dot_general | solution.py:19
  181.0 16.6 %copy = bf16[3072,2048]{1,0:T(8,128)(2,1)} copy(bf16[3072,2048]{0,1:T(8,128)(2,1)} %convert_bitcast_fusion.1) | data formatting | bytes 25165824
  197.6 34.1 %convert_bitcast_fusion = bf16[3072,2048]{0,1:T(8,128)(2,1)} fusion(bf16[1408,3072]{1,0:T(8,128)(2,1)} %all-gather.13.cloned.1.call-done, f32[1408,2048]{1,0:T(8,128)} %get-tuple-element.5, bf16[1408,2048]{1,0:T(8,128)(2,1)} %param.3), kind=kOutput, calls=%fused_computation.6 | convolution fusion | flops 17743216640 | bytes 38535168 | tf_op jit(solution)/gta,gtb->gab/dot_general | solution.py:19
  231.7 16.6 %copy.1 = bf16[3072,2048]{1,0:T(8,128)(2,1)} copy(bf16[3072,2048]{0,1:T(8,128)(2,1)} %convert_bitcast_fusion) | data formatting | bytes 25165824
  248.3 33.9 %convolution_convert_fusion = bf16[2048,3072]{1,0:T(8,128)(2,1)} fusion(bf16[1408,3072]{1,0:T(8,128)(2,1)} %all-gather.11.cloned.1.call-done, bf16[1408,2048]{1,0:T(8,128)(2,1)} %param.2, bf16[1408,2048]{1,0:T(8,128)(2,1)} %param.3), kind=kOutput, calls=%fused_computation.16 | convolution fusion | flops 17746100224 | bytes 32768000 | tf_op jit(solution)/gta,gtb->gab/dot_general | solution.py:19
  282.3 0.0 reduce-scatter.4.cloned.1.call-done
Async XLA Ops:
  7.2 62.4 %all-gather.11.cloned.1.call-start = ((), (), s32[]{:S(2)}) async-start(), calls=%async_computation.1 | async-start | bytes 10813440 | tf_op args[1]
  7.9 147.2 %all-gather.13.cloned.1.call-start = ((), (), s32[]{:S(2)}) async-start(), calls=%async_computation.2 | async-start | bytes 10813440 | tf_op jit(solution)/reshape | solution.py:18
  8.6 273.6 %reduce-scatter.4.cloned.1.call-start = ((), (), s32[]{:S(2)}) async-start(), calls=%async_computation.3 | async-start | bytes 10813440
  99.8 24.3 %copy-start = (bf16[1408,2048]{1,0:T(8,128)(2,1)}, bf16[1408,2048]{1,0:T(8,128)(2,1)S(1)}, u32[]{:S(2)}) copy-start(bf16[1408,2048]{1,0:T(8,128)(2,1)S(1)} %get-tuple-element.4) | copy-start | bytes 17301508
Sparse Core Ops, SparseCore 0:
  9.5 60.0 all-gather.10
  71.1 57.2 all-gather.12
  155.2 66.6 reduce-scatter.3
where the time goes:
time: 290 us; the launch traced here: 289 us
  matrix products  179 us (62%)
  waiting for transfers between devices  62.3 us (21%)
  local copies, waits for them, and re-layouts  33.2 us (11%)
  between operations  13.8 us (5%)
    dot_general x3, matrix products, by_group(): jnp.einsum('gta,gtb->gab', a, b, preferred_element_type=jnp.float32)  94 us
    unnamed x5, waiting for transfers between devices  62.3 us
    dot_general x2, matrix products, step(): dx = jnp.dot(d_gate, w_gate.T) + jnp.dot(d_up, w_up.T)  55.2 us
    unnamed x4, local copies, waits for them, and re-layouts  33.2 us
    dot_general x1, matrix products, step(): d_hidden = jnp.dot(dy, w_down.T, preferred_element_type=jnp.float32)  30.2 us
  transfers between devices with their start and end apart: 3, of which 1 were waited for; matrix products, arithmetic and copies ran while one was open for 74% of the time, Pallas kernels for 0%

commit v1 on v0

v1 whole, which is shorter than its diff:
```python
import functools

import jax
import jax.numpy as jnp
from jax import lax
from jax.experimental import pallas as pl
from jax.experimental.pallas import tpu as pltpu
from jax.sharding import PartitionSpec as P

F32 = jnp.float32
BF16 = jnp.bfloat16
DMA = pltpu.SemaphoreType.DMA
ANY = pl.BlockSpec(memory_space=pl.ANY)
VMEM_LIMIT = 60 * 2**20


def nt(a, b):
    return lax.dot_general(a, b, (((1,), (1,)), ((), ())), preferred_element_type=F32)


def tn(a, b):
    return lax.dot_general(a, b, (((0,), (0,)), ((), ())), preferred_element_type=F32)


def hidden_grads_kernel(dy_a, dy_b, w_down, gate, up, w_gate, w_up, *rest, slot, row, bn, bx, n_alias):
    (d_gate, d_up, hidden, keep, send), scratch = rest[n_alias : n_alias + 5], rest[n_alias + 5 :]
    (dyv, wdb, gb, ub, da, db, dgv, duv, hv, wgb, wub, kb, sb, s_dy, s_w, s_g, s_u, s_x, s_o, s_k, s_s) = scratch
    rows, depth = dyv.shape
    half = rows // 2
    ff = w_down.shape[0]
    steps, blocks = ff // bn, depth // bx
    sub = bn // 2
    me = lax.axis_index("tp")

    def at(k):
        return pl.multiple_of(row(me, k), 16)

    def dy_copy(k):
        return pltpu.make_async_copy((dy_a, dy_b)[k], dyv.at[pl.ds(k * half, half)], s_dy.at[k])

    def w_copy(j, b):
        return pltpu.make_async_copy(w_down.at[pl.ds(pl.multiple_of(j * bn, bn), bn)], wdb.at[b], s_w.at[b])

    def act_copies(j, b):
        cols = pl.ds(pl.multiple_of(j * bn, bn), bn)
        return [
            pltpu.make_async_copy(src.at[pl.ds(at(k), half), cols], buf.at[b, pl.ds(k * half, half)], sem.at[b, k])
            for src, buf, sem in ((gate, gb, s_g), (up, ub, s_u))
            for k in range(2)
        ]

    def x_copies(i, b):
        r = pl.ds(pl.multiple_of(i * bx, bx), bx)
        return [
            pltpu.make_async_copy(w_gate.at[r], wgb.at[b], s_x.at[0, b]),
            pltpu.make_async_copy(w_up.at[r], wub.at[b], s_x.at[1, b]),
        ]

    def out_copies(i, b):
        c = pl.ds(pl.multiple_of(i * bx, bx), bx)
        return [
            pltpu.make_async_copy(kb.at[b], keep.at[:, c], s_k.at[b]),
            pltpu.make_async_copy(sb.at[b], send.at[:, c], s_s.at[b]),
        ]

    def epilogue(d, j, b, part):
        s = pl.ds(part * sub, sub)
        g, u = gb[b, :, s].astype(F32), ub[b, :, s].astype(F32)
        sig = 1.0 / (1.0 + jnp.exp(-g))
        silu = g * sig
        dh = d[...]
        o = pl.ds(pl.multiple_of(j * bn + part * sub, sub), sub)
        hv[:, o] = (silu * u).astype(BF16)
        duv[:, o] = (dh * silu).astype(BF16)
        dgv[:, o] = ((dh * u) * (sig + silu * (1.0 - sig))).astype(BF16)

    def start(copies):
        for c in copies:
            c.start()

    def wait(copies):
        for c in copies:
            c.wait()

    dy_copy(0).start()
    dy_copy(1).start()
    w_copy(0, 0).start()
    start(act_copies(0, 0))
    dy_copy(0).wait()
    dy_copy(1).wait()

    def step(j, carry):
        b, b3 = lax.rem(j, 2), lax.rem(j, 3)
        w_copy(j, b).wait()
        wait(act_copies(j, b3))

        @pl.when(j + 1 < steps)
        def _():
            w_copy(j + 1, 1 - b).start()
            start(act_copies(j + 1, lax.rem(j + 1, 3)))

        @pl.when(j + 1 == steps)
        def _():
            start(x_copies(0, 0))

        da[...] = nt(dyv[...], wdb[b, pl.ds(0, sub)])
        epilogue(db, jnp.maximum(j - 1, 0), lax.rem(j + 2, 3), 1)
        db[...] = nt(dyv[...], wdb[b, pl.ds(sub, sub)])
        epilogue(da, j, b3, 0)
        return carry

    lax.fori_loop(0, steps, step, 0)
    epilogue(db, steps - 1, (steps - 1) % 3, 1)
    saved = [
        pltpu.make_async_copy(v, o.at[pl.ds(slot, rows)], s_o.at[n])
        for n, (v, o) in enumerate(((dgv, d_gate), (duv, d_up), (hv, hidden)))
    ]
    start(saved)

    def block(i, carry):
        b = lax.rem(i, 2)
        wait(x_copies(i, b))

        @pl.when(i + 1 < blocks)
        def _():
            start(x_copies(i + 1, 1 - b))

        @pl.when(i >= 2)
        def _():
            wait(out_copies(i - 2, b))

        t = nt(dgv[...], wgb[b]) + nt(duv[...], wub[b])
        kb[b] = t[:half]
        sb[b] = t[half:].astype(BF16)
        start(out_copies(i, b))
        return carry

    lax.fori_loop(0, blocks, block, 0)
    for i in (blocks - 2, blocks - 1):
        wait(out_copies(i, i % 2))
    wait(saved)


def hidden_grads(dy_a, dy_b, w_down, gate, up, w_gate, w_up, into, *, slot, row, bn=512, bx=512, name):
    half, depth = dy_a.shape
    rows, (total, ff) = 2 * half, gate.shape
    S = jax.ShapeDtypeStruct
    n_alias = len(into)
    V = pltpu.VMEM
    return pl.pallas_call(
        functools.partial(hidden_grads_kernel, slot=slot, row=row, bn=bn, bx=bx, n_alias=n_alias),
        in_specs=[ANY] * (7 + n_alias),
        out_specs=[ANY] * 5,
        out_shape=[S((total, ff), BF16)] * 3 + [S((half, depth), F32), S((half, depth), BF16)],
        scratch_shapes=[
            V((rows, depth), BF16), V((2, bn, depth), BF16), V((3, rows, bn), BF16), V((3, rows, bn), BF16),
            V((rows, bn // 2), F32), V((rows, bn // 2), F32), V((rows, ff), BF16), V((rows, ff), BF16), V((rows, ff), BF16),
            V((2, bx, ff), BF16), V((2, bx, ff), BF16), V((2, half, bx), F32), V((2, half, bx), BF16),
            DMA((2,)), DMA((2,)), DMA((3, 2)), DMA((3, 2)), DMA((2, 2)), DMA((3,)), DMA((2,)), DMA((2,)),
        ],
        input_output_aliases={7 + n: n for n in range(n_alias)},
        compiler_params=pltpu.CompilerParams(vmem_limit_bytes=VMEM_LIMIT),
        cost_estimate=pl.CostEstimate(
            flops=6 * rows * depth * ff, bytes_accessed=6 * depth * ff, transcendentals=rows * ff
        ),
        name=name,
    )(dy_a, dy_b, w_down, gate, up, w_gate, w_up, *into)


def weight_grads_kernel(*refs, left, right, n_left, n_right, n_out, bm, bc):
    lefts, rights = refs[:n_left], refs[n_left : n_left + n_right]
    outs = refs[n_left + n_right : n_left + n_right + n_out]
    lb, rv, ob, s_l, s_r, s_o = refs[n_left + n_right + n_out :]
    m = lefts[0].shape[1]
    n = rv.shape[2]
    blocks, chunks = m // bm, n // bc

    def l_copies(i, b):
        c = pl.ds(pl.multiple_of(i * bm, bm), bm)
        return [
            pltpu.make_async_copy(
                lefts[p].at[pl.ds(r0, rows), c], lb.at[b, pl.ds(to, rows)], s_l.at[b, k]
            )
            for k, (p, r0, to, rows) in enumerate(left)
        ]

    def r_copies(r, c):
        cc = pl.ds(c * bc, bc)
        return [
            pltpu.make_async_copy(
                rights[p].at[pl.ds(r0, rows), cc], rv.at[r, pl.ds(to, rows), cc], s_r.at[r, c, k]
            )
            for k, (p, r0, to, rows) in enumerate(right[r])
        ]

    def o_copy(r, i, b):
        return pltpu.make_async_copy(ob.at[b, r], outs[r].at[pl.ds(pl.multiple_of(i * bm, bm), bm)], s_o.at[b, r])

    def start(copies):
        for c in copies:
            c.start()

    def wait(copies):
        for c in copies:
            c.wait()

    pieces = [(r, c) for r in range(n_out) for c in range(chunks)]
    start(l_copies(0, 0))
    for r, c in pieces:
        start(r_copies(r, c))

    wait(l_copies(0, 0))
    start(l_copies(1, 1))
    for r, c in pieces:
        wait(r_copies(r, c))
        cc = pl.ds(c * bc, bc)
        ob[0, r, :, cc] = tn(lb[0], rv[r, :, cc]).astype(BF16)
    for r in range(n_out):
        o_copy(r, 0, 0).start()

    def block(i, carry):
        b = lax.rem(i, 2)
        wait(l_copies(i, b))

        @pl.when(i + 1 < blocks)
        def _():
            start(l_copies(i + 1, 1 - b))

        @pl.when(i >= 2)
        def _():
            for r in range(n_out):
                o_copy(r, i - 2, b).wait()

        for r in range(n_out):
            ob[b, r] = tn(lb[b], rv[r]).astype(BF16)
        for r in range(n_out):
            o_copy(r, i, b).start()
        return carry

    lax.fori_loop(1, blocks, block, 0)
    for i in (blocks - 2, blocks - 1):
        for r in range(n_out):
            o_copy(r, i, i % 2).wait()


def weight_grads(lefts, left, rights, right, *, bm, bc, name):
    n_out = len(right)
    total = sum(p[3] for p in left)
    m, n = lefts[0].shape[1], rights[0].shape[1]
    V = pltpu.VMEM
    return pl.pallas_call(
        functools.partial(
            weight_grads_kernel, left=left, right=right, n_left=len(lefts), n_right=len(rights), n_out=n_out, bm=bm, bc=bc
        ),
        in_specs=[ANY] * (len(lefts) + len(rights)),
        out_specs=[ANY] * n_out,
        out_shape=[jax.ShapeDtypeStruct((m, n), BF16)] * n_out,
        scratch_shapes=[
            V((2, total, bm), BF16), V((n_out, total, n), BF16), V((2, n_out, bm, n), BF16),
            DMA((2, len(left))), DMA((n_out, n // bc, max(len(r) for r in right))), DMA((2, n_out)),
        ],
        compiler_params=pltpu.CompilerParams(vmem_limit_bytes=VMEM_LIMIT),
        cost_estimate=pl.CostEstimate(flops=2 * n_out * total * m * n, bytes_accessed=2 * n_out * m * n, transcendentals=0),
        name=name,
    )(*lefts, *rights)


def finish_kernel(chip, part, *rest):
    out = rest[-1]
    out[...] = (chip[...] + part[...].astype(F32)).astype(BF16)


def finish(chip, part, k, into, *, name):
    h, depth = part.shape
    bc = 1024
    whole = pl.BlockSpec((h, bc), lambda c: (k, c))
    return pl.pallas_call(
        finish_kernel,
        grid=(depth // bc,),
        in_specs=[whole, pl.BlockSpec((h, bc), lambda c: (0, c))] + [ANY] * len(into),
        out_specs=whole,
        out_shape=jax.ShapeDtypeStruct(chip.shape, BF16),
        input_output_aliases={2: 0} if into else {},
        cost_estimate=pl.CostEstimate(flops=h * depth, bytes_accessed=8 * h * depth, transcendentals=0),
        compiler_params=pltpu.CompilerParams(vmem_limit_bytes=16 * 2**20),
        name=name,
    )(chip, part, *into)


def solution(mesh):
    mate = [(i, i ^ 1) for i in range(4)]
    across = [(i, i ^ 2) for i in range(4)]

    def step(x, dy, gate, up, w_gate, w_up, w_down):
        own = dy.shape[0]
        h = own // 2
        to_mate = lambda a: lax.ppermute(a, "tp", mate)
        to_across = lambda a: lax.ppermute(a, "tp", across)
        tie = lax.optimization_barrier

        dy_q = [to_across(dy[k * h : (k + 1) * h]) for k in range(2)]
        dy_mate = to_mate(dy)
        x_q = [to_across(x[k * h : (k + 1) * h]) for k in range(2)]
        x_mate = to_mate(x)

        weights = (w_down, gate, up, w_gate, w_up)
        *saved, keep, send = hidden_grads(
            dy, dy_mate, *weights, (), slot=0, row=lambda me, k: (me ^ k) * own, name="local"
        )
        parts, dy_r, x_r = [], [None] * 2, [None] * 2
        q, saved, keep, send = tie((dy_q[0], saved, keep, send))
        dy_q[0], dy_r[0] = q, to_mate(q)
        chip = keep + to_mate(send).astype(F32)
        for k in range(2):
            saved, chip, dy_r[k] = tie((saved, chip, dy_r[k]))
            *saved, keep, send = hidden_grads(
                dy_q[k], dy_r[k], *weights, saved, slot=2 * own + 2 * h * k,
                row=lambda me, s, k=k: (me ^ 2 ^ s) * own + k * h, name=f"remote{k}",
            )
            if k == 0:
                q, saved, keep, send = tie((dy_q[1], saved, keep, send))
                dy_q[1], dy_r[1] = q, to_mate(q)
            else:
                q, saved, keep, send = tie((x_q[0], saved, keep, send))
                x_q[0], x_r[0] = q, to_mate(q)
            pair = (keep + to_mate(send).astype(F32)).astype(BF16)
            parts.append(to_across(pair))
        d_gate, d_up, hidden = saved

        slots = [(0, 0, 0, own), (1, 0, own, own)]
        dy_slots = slots + [(2 + i, 0, 2 * own + i * h, h) for i in range(4)]
        whole = [(0, 0, 0, 4 * own)]
        hidden, x_r[0] = tie((hidden, x_r[0]))
        (dw_down,) = weight_grads(
            (hidden,), whole, (dy, dy_mate, dy_q[0], dy_r[0], dy_q[1], dy_r[1]), [dy_slots], bm=512, bc=1024, name="down"
        )
        q, dw_down, d_gate, d_up = tie((x_q[1], dw_down, d_gate, d_up))
        x_q[1], x_r[1] = q, to_mate(q)
        dw_gate, dw_up = weight_grads(
            (x, x_mate, x_q[0], x_r[0], x_q[1], x_r[1]), dy_slots, (d_gate, d_up), [whole, [(1, 0, 0, 4 * own)]], bm=512,
            bc=1024, name="gateup"
        )
        parts, chip, dw_gate, dw_up = tie((parts, chip, dw_gate, dw_up))
        dx = finish(chip, parts[0], 0, (), name="finish0")
        dx = finish(chip, parts[1], 1, (dx,), name="finish1")
        return dx, dw_gate, dw_up, dw_down

    rows, cols = P(("dp", "tp"), None), P("dp", "tp")
    return jax.shard_map(
        step,
        mesh=mesh,
        in_specs=(rows, rows, cols, cols, P(None, "tp"), P(None, "tp"), P("tp", None)),
        out_specs=(rows, cols, cols, rows),
        check_vma=False,
    )
```

time: 290 us -> 207 us (0.71)
  matrix products: 179 us -> 0 us
  Pallas kernels: 0 us -> 173 us
  waiting for transfers between devices: 62.3 us -> 3.36 us
  local copies, waits for them, and re-layouts: 33.2 us -> 9.78 us
  between operations: 13.8 us -> 0.79 us
  starting transfers between devices: 0.11 us -> 11 us
  other arithmetic: 0 us -> 9.09 us
    dot_general x6 -> x0, matrix products: 179 us -> none  [the longest x3 94 us: by_group(): jnp.einsum('gta,gtb->gab', a, b, preferred_element_type=jnp.float32)]
    pallas_call x0 -> x7, Pallas kernels: none -> 173 us  [the longest x3 95.9 us: hidden_grads(): pl.pallas_call(functools.partial(hidden_grads_kernel, slot=slot, row=row,...]
    unnamed x5 -> x0, waiting for transfers between devices: 62.3 us -> none
    unnamed x4 -> x14, local copies, waits for them, and re-layouts: 33.2 us -> 4.28 us
    ppermute x0 -> x15, starting transfers between devices: none -> 11 us  [the longest x6 8.08 us: step(): to_across = lambda a: lax.ppermute(a, 'tp', across)]
    slice x0 -> x2, local copies, waits for them, and re-layouts: none -> 5.51 us  [the longest x1 2.83 us: step(): x_q = [to_across(x[k * h:(k + 1) * h]) for k in range(2)]]
    add x0 -> x1, other arithmetic: none -> 4.99 us  [step(): chip = keep + to_mate(send).astype(F32)]
    convert_element_type x0 -> x2, other arithmetic: none -> 4.1 us  [step(): pair = (keep + to_mate(send).astype(F32)).astype(BF16)]
  transfers between devices with their start and end apart: 3 -> 15, of which waited for: 1 -> 2; matrix products, arithmetic and copies ran while one was open for 74% -> 7% of each run, Pallas kernels for 0% -> 82%
where the time goes in v1:
time: 207 us
  Pallas kernels  173 us (84%)
  starting transfers between devices  11 us (5%)
  local copies, waits for them, and re-layouts  9.78 us (5%)
  other arithmetic  9.09 us (4%)
  waiting for transfers between devices  3.36 us (2%)
    pallas_call x3, Pallas kernels, hidden_grads(): pl.pallas_call(functools.partial(hidden_grads_kernel, slot=slot, row=row,...  95.9 us
    pallas_call x2, Pallas kernels, weight_grads(): pl.pallas_call(functools.partial(weight_grads_kernel, left=left, right=ri...  73.5 us
    ppermute x6, starting transfers between devices, step(): to_across = lambda a: lax.ppermute(a, 'tp', across)  8.08 us
    add x1, other arithmetic, step(): chip = keep + to_mate(send).astype(F32)  4.99 us
    unnamed x14, local copies, waits for them, and re-layouts  4.28 us
  transfers between devices with their start and end apart: 15, of which 2 were waited for; matrix products, arithmetic and copies ran while one was open for 7% of the time, Pallas kernels for 82%

profile of v1, /device:TPU:0, one launch (start us, length us, event | category | flops | bytes accessed | tf_op | source)
XLA Modules:
  0.0 206.9 jit_solution(11030496709639335829)
XLA Ops:
  0.6 0.9 collective-permute-start.2
  1.5 2.7 %fusion.1 = (bf16[176,3072]{1,0:T(8,128)(2,1)S(1)}, bf16[176,3072]{1,0:T(8,128)(2,1)}) fusion(bf16[352,3072]{1,0:T(8,128)(2,1)} %refs_1_.1), kind=kLoop, calls=%fused_computation.4 | loop fusion | bytes 4325376 | tf_op jit(solution)/shard_map/slice | solution.py:301
  4.2 2.5 %collective-permute-start.1 = (bf16[176,3072]{1,0:T(8,128)(2,1)S(1)}, bf16[176,3072]{1,0:T(8,128)(2,1)S(1)}, u32[]{:S(2)}, u32[]{:S(2)}) collective-permute-start(bf16[176,3072]{1,0:T(8,128)(2,1)S(1)} %get-tuple-element.118), channel_id=1, source_target_pairs={{0,2},{1,3},{2,0},{3,1},{4,6},{5,7},{6,4},{7,5}} | collective-permute-start | bytes 3244040 | tf_op jit(solution)/shard_map/ppermute | solution.py:298
  6.7 0.0 collective-permute-done.2.dy_b.refs_2_
  6.7 39.5 %local.1 = (bf16[1408,2048]{1,0:T(8,128)(2,1)}, bf16[1408,2048]{1,0:T(8,128)(2,1)}, bf16[1408,2048]{1,0:T(8,128)(2,1)}, f32[352,3072]{1,0:T(8,128)}, bf16[352,3072]{1,0:T(8,128)(2,1)}) custom-call(bf16[352,3072]{1,0:T(8,128)(2,1)} %refs_1_.1, bf16[352,3072]{1,0:T(8,128)(2,1)} %collective-permute-done.2.dy_b.refs_2_, bf16[2048,3072]{1,0:T(8,128)(2,1)} %w_down.5, ...), custom_call_target="tpu_custom_call" | custom-call | flops 26575110144 | bytes 37748736 | tf_op jit(solution)/shard_map/local/pallas_call | solution.py:150
  46.2 0.0 collective-permute-done.1.dy_a.refs_3_
  46.2 0.0 copy-start.3
  46.2 0.2 collective-permute-start.3
  46.4 0.3 collective-permute-start.4
  46.7 1.5 collective-permute-start
  48.2 2.2 %collective-permute-done.3 = bf16[352,3072]{1,0:T(8,128)(2,1)S(1)} collective-permute-done((bf16[352,3072]{1,0:T(8,128)(2,1)}, bf16[352,3072]{1,0:T(8,128)(2,1)S(1)}, u32[]{:S(2)}, u32[]{:S(2)}) %collective-permute-start.3) | collective-permute-done | bytes 2162720 | tf_op jit(solution)/shard_map/ppermute | solution.py:297
  50.5 5.0 %convert_add_fusion.chip = f32[352,3072]{1,0:T(8,128)} fusion(f32[352,3072]{1,0:T(8,128)} %get-tuple-element.69, bf16[352,3072]{1,0:T(8,128)(2,1)S(1)} %collective-permute-done.3), kind=kLoop, calls=%fused_computation | loop fusion | flops 2162688 | bytes 10813440 | tf_op jit(solution)/shard_map/add | solution.py:313
  55.5 0.0 copy-done.3
  55.5 0.0 collective-permute-done.4.dy_b.refs_4_
  55.5 1.0 copy-done.4
  56.5 28.2 %remote0.1 = (bf16[1408,2048]{1,0:T(8,128)(2,1)}, bf16[1408,2048]{1,0:T(8,128)(2,1)}, bf16[1408,2048]{1,0:T(8,128)(2,1)}, f32[176,3072]{1,0:T(8,128)}, bf16[176,3072]{1,0:T(8,128)(2,1)}) custom-call(bf16[176,3072]{1,0:T(8,128)(2,1)} %copy-done.3, bf16[176,3072]{1,0:T(8,128)(2,1)} %copy-done.4, ...), custom_call_target="tpu_custom_call", output_to_operand_aliasing={{0}: (7, {}), {1}: (8, {}), {2}: (9, {})} | custom-call | flops 13287555072 | bytes 37748736 | tf_op jit(solution)/shard_map/remote0/pallas_call | solution.py:150
  84.7 0.0 collective-permute-done.dy_a.refs_5_
  84.7 0.2 collective-permute-start.8
  84.9 2.8 %fusion = (bf16[176,3072]{1,0:T(8,128)(2,1)S(1)}, bf16[176,3072]{1,0:T(8,128)(2,1)}) fusion(bf16[352,3072]{1,0:T(8,128)(2,1)} %refs_0_.1), kind=kLoop, calls=%fused_computation.3 | loop fusion | bytes 4325376 | tf_op jit(solution)/shard_map/slice | solution.py:303
  87.7 1.5 collective-permute-start.7
  89.2 0.0 collective-permute-done.8.dy_b.refs_6_
  89.2 1.1 copy-done.6
  90.3 28.2 %remote1.1 = (bf16[1408,2048]{1,0:T(8,128)(2,1)}, bf16[1408,2048]{1,0:T(8,128)(2,1)}, bf16[1408,2048]{1,0:T(8,128)(2,1)}, f32[176,3072]{1,0:T(8,128)}, bf16[176,3072]{1,0:T(8,128)(2,1)}) custom-call(bf16[176,3072]{1,0:T(8,128)(2,1)} %copy-done.5, bf16[176,3072]{1,0:T(8,128)(2,1)} %copy-done.6, ...), custom_call_target="tpu_custom_call", output_to_operand_aliasing={{0}: (7, {}), {1}: (8, {}), {2}: (9, {})} | custom-call | flops 13287555072 | bytes 37748736 | tf_op jit(solution)/shard_map/remote1/pallas_call | solution.py:150
  118.5 0.0 collective-permute-done.7.refs_2_
  118.5 0.0 collective-permute-start.12
  118.5 0.5 collective-permute-start.11
  119.0 0.5 collective-permute-start.13
  119.6 0.0 collective-permute-start.5
  119.6 0.5 collective-permute-start.9
  120.1 1.1 collective-permute-done.12.refs_3_
  121.2 26.4 %down.1 = bf16[2048,3072]{1,0:T(8,128)(2,1)} custom-call(bf16[1408,2048]{1,0:T(8,128)(2,1)} %get-tuple-element.102.refs_0_, bf16[352,3072]{1,0:T(8,128)(2,1)} %refs_1_.1, bf16[352,3072]{1,0:T(8,128)(2,1)} %collective-permute-done.2.dy_b.refs_2_, bf16[176,3072]{1,0:T(8,128)(2,1)} %copy-done.3, bf16[176,3072]{1,0:T(8,128)(2,1)} %copy-done.4, ...), custom_call_target="tpu_custom_call" | custom-call | flops 17716740096 | bytes 12582912 | tf_op jit(solution)/shard_map/down/pallas_call | solution.py:251
  147.6 0.0 copy-start.2
  147.6 0.0 collective-permute-done.13.refs_4_
  147.6 0.2 collective-permute-start.14
  147.8 0.0 collective-permute-done.5
  147.8 2.6 %add_convert_fusion.1 = bf16[176,3072]{1,0:T(8,128)(2,1)} fusion(f32[176,3072]{1,0:T(8,128)S(1)} %copy-done.1, bf16[176,3072]{1,0:T(8,128)(2,1)} %collective-permute-done.5), kind=kLoop, calls=%fused_computation.2 | loop fusion | flops 1622016 | bytes 4325376 | tf_op jit(solution)/shard_map/convert_element_type | solution.py:326
  150.4 0.6 collective-permute-start.6
  151.0 0.0 collective-permute-done.9
  151.0 1.5 add_convert_fusion
  152.5 1.5 collective-permute-start.10
  154.0 0.0 collective-permute-done.11.refs_1_
  154.0 0.0 collective-permute-done.14.refs_5_
  154.0 47.1 %gateup.1 = (bf16[3072,2048]{1,0:T(8,128)(2,1)}, bf16[3072,2048]{1,0:T(8,128)(2,1)}) custom-call(bf16[352,3072]{1,0:T(8,128)(2,1)} %refs_0_.1, bf16[352,3072]{1,0:T(8,128)(2,1)} %collective-permute-done.11.refs_1_, bf16[176,3072]{1,0:T(8,128)(2,1)} %collective-permute-done.7.refs_2_, bf16[176,3072]{1,0:T(8,128)(2,1)} %collective-permute-done.12.refs_3_, ...), custom_call_target="tpu_custom_call" | custom-call | flops 35433480192 | bytes 25165824 | tf_op jit(solution)/shard_map/gateup/pallas_call | solution.py:251
  201.1 0.0 collective-permute-done.6.part
  201.1 0.0 collective-permute-done.10.part
  201.1 2.2 %copy-done = f32[352,3072]{1,0:T(8,128)S(1)} copy-done((f32[352,3072]{1,0:T(8,128)S(1)}, f32[352,3072]{1,0:T(8,128)}, u32[]{:S(2)}) %copy-start) | copy-done | bytes 4325400
  203.3 1.8 finish0.1.rest_0_
  205.1 1.8 finish1.1
  (8 shorter events, 0.0 us)
Async XLA Ops:
  0.6 6.1 %collective-permute-start.2 = (bf16[352,3072]{1,0:T(8,128)(2,1)}, bf16[352,3072]{1,0:T(8,128)(2,1)}, u32[]{:S(2)}, u32[]{:S(2)}) collective-permute-start(bf16[352,3072]{1,0:T(8,128)(2,1)} %refs_1_.1), channel_id=1, source_target_pairs={{0,1},{1,0},{2,3},{3,2},{4,5},{5,4},{6,7},{7,6}} | collective-permute-start | bytes 6488072 | tf_op jit(solution)/shard_map/ppermute | solution.py:297
  4.2 42.0 %collective-permute-start.1 = (bf16[176,3072]{1,0:T(8,128)(2,1)S(1)}, bf16[176,3072]{1,0:T(8,128)(2,1)S(1)}, u32[]{:S(2)}, u32[]{:S(2)}) collective-permute-start(bf16[176,3072]{1,0:T(8,128)(2,1)S(1)} %get-tuple-element.118), channel_id=1, source_target_pairs={{0,2},{1,3},{2,0},{3,1},{4,6},{5,7},{6,4},{7,5}} | collective-permute-start | bytes 3244040 | tf_op jit(solution)/shard_map/ppermute | solution.py:298
  46.2 9.3 %copy-start.3 = (bf16[176,3072]{1,0:T(8,128)(2,1)}, bf16[176,3072]{1,0:T(8,128)(2,1)S(1)}, u32[]{:S(2)}) copy-start(bf16[176,3072]{1,0:T(8,128)(2,1)S(1)} %collective-permute-done.1.dy_a.refs_3_) | copy-start | bytes 3244036
  46.2 4.3 %collective-permute-start.3 = (bf16[352,3072]{1,0:T(8,128)(2,1)}, bf16[352,3072]{1,0:T(8,128)(2,1)S(1)}, u32[]{:S(2)}, u32[]{:S(2)}) collective-permute-start(bf16[352,3072]{1,0:T(8,128)(2,1)} %get-tuple-element.70), channel_id=1, source_target_pairs={{0,1},{1,0},{2,3},{3,2},{4,5},{5,4},{6,7},{7,6}} | collective-permute-start | bytes 6488072 | tf_op jit(solution)/shard_map/ppermute | solution.py:297
  46.4 9.0 %collective-permute-start.4 = (bf16[176,3072]{1,0:T(8,128)(2,1)S(1)}, bf16[176,3072]{1,0:T(8,128)(2,1)S(1)}, u32[]{:S(2)}, u32[]{:S(2)}) collective-permute-start(bf16[176,3072]{1,0:T(8,128)(2,1)S(1)} %collective-permute-done.1.dy_a.refs_3_), channel_id=1, source_target_pairs={{0,1},{1,0},{2,3},{3,2},{4,5},{5,4},{6,7},{7,6}} | collective-permute-start | bytes 3244040 | tf_op jit(solution)/shard_map/ppermute | solution.py:297
  46.7 37.9 %collective-permute-start = (bf16[176,3072]{1,0:T(8,128)(2,1)}, bf16[176,3072]{1,0:T(8,128)(2,1)S(1)}, u32[]{:S(2)}, u32[]{:S(2)}) collective-permute-start(bf16[176,3072]{1,0:T(8,128)(2,1)} %get-tuple-element.119), channel_id=1, source_target_pairs={{0,2},{1,3},{2,0},{3,1},{4,6},{5,7},{6,4},{7,5}} | collective-permute-start | bytes 3244040 | tf_op jit(solution)/shard_map/ppermute | solution.py:298
  55.5 1.0 copy-start.4
  84.7 3.1 %copy-start.5 = (bf16[176,3072]{1,0:T(8,128)(2,1)}, bf16[176,3072]{1,0:T(8,128)(2,1)S(1)}, u32[]{:S(2)}) copy-start(bf16[176,3072]{1,0:T(8,128)(2,1)S(1)} %collective-permute-done.dy_a.refs_5_) | copy-start | bytes 3244036
  84.7 4.6 %collective-permute-start.8 = (bf16[176,3072]{1,0:T(8,128)(2,1)S(1)}, bf16[176,3072]{1,0:T(8,128)(2,1)S(1)}, u32[]{:S(2)}, u32[]{:S(2)}) collective-permute-start(bf16[176,3072]{1,0:T(8,128)(2,1)S(1)} %collective-permute-done.dy_a.refs_5_), channel_id=1, source_target_pairs={{0,1},{1,0},{2,3},{3,2},{4,5},{5,4},{6,7},{7,6}} | collective-permute-start | bytes 3244040 | tf_op jit(solution)/shard_map/ppermute | solution.py:297
  87.7 30.8 %collective-permute-start.7 = (bf16[176,3072]{1,0:T(8,128)(2,1)}, bf16[176,3072]{1,0:T(8,128)(2,1)}, u32[]{:S(2)}, u32[]{:S(2)}) collective-permute-start(bf16[176,3072]{1,0:T(8,128)(2,1)} %get-tuple-element.117), channel_id=1, source_target_pairs={{0,2},{1,3},{2,0},{3,1},{4,6},{5,7},{6,4},{7,5}} | collective-permute-start | bytes 3244040 | tf_op jit(solution)/shard_map/ppermute | solution.py:298
  89.2 1.1 copy-start.6
  118.5 2.7 %collective-permute-start.12 = (bf16[176,3072]{1,0:T(8,128)(2,1)}, bf16[176,3072]{1,0:T(8,128)(2,1)}, u32[]{:S(2)}, u32[]{:S(2)}) collective-permute-start(bf16[176,3072]{1,0:T(8,128)(2,1)} %collective-permute-done.7.refs_2_), channel_id=1, source_target_pairs={{0,1},{1,0},{2,3},{3,2},{4,5},{5,4},{6,7},{7,6}} | collective-permute-start | bytes 3244040 | tf_op jit(solution)/shard_map/ppermute | solution.py:297
  118.5 35.5 %collective-permute-start.11 = (bf16[352,3072]{1,0:T(8,128)(2,1)}, bf16[352,3072]{1,0:T(8,128)(2,1)}, u32[]{:S(2)}, u32[]{:S(2)}) collective-permute-start(bf16[352,3072]{1,0:T(8,128)(2,1)} %refs_0_.1), channel_id=1, source_target_pairs={{0,1},{1,0},{2,3},{3,2},{4,5},{5,4},{6,7},{7,6}} | collective-permute-start | bytes 6488072 | tf_op jit(solution)/shard_map/ppermute | solution.py:297
  119.0 28.8 %copy-start.1 = (f32[176,3072]{1,0:T(8,128)S(1)}, f32[176,3072]{1,0:T(8,128)}, u32[]{:S(2)}) copy-start(f32[176,3072]{1,0:T(8,128)} %get-tuple-element.80) | copy-start | bytes 6488068
  119.0 28.6 %collective-permute-start.13 = (bf16[176,3072]{1,0:T(8,128)(2,1)S(1)}, bf16[176,3072]{1,0:T(8,128)(2,1)}, u32[]{:S(2)}, u32[]{:S(2)}) collective-permute-start(bf16[176,3072]{1,0:T(8,128)(2,1)S(1)} %get-tuple-element.116), channel_id=1, source_target_pairs={{0,2},{1,3},{2,0},{3,1},{4,6},{5,7},{6,4},{7,5}} | collective-permute-start | bytes 3244040 | tf_op jit(solution)/shard_map/ppermute | solution.py:298
  119.6 28.2 %collective-permute-start.5 = (bf16[176,3072]{1,0:T(8,128)(2,1)}, bf16[176,3072]{1,0:T(8,128)(2,1)}, u32[]{:S(2)}, u32[]{:S(2)}) collective-permute-start(bf16[176,3072]{1,0:T(8,128)(2,1)} %get-tuple-element.81), channel_id=1, source_target_pairs={{0,1},{1,0},{2,3},{3,2},{4,5},{5,4},{6,7},{7,6}} | collective-permute-start | bytes 3244040 | tf_op jit(solution)/shard_map/ppermute | solution.py:297
  119.6 31.4 %collective-permute-start.9 = (bf16[176,3072]{1,0:T(8,128)(2,1)}, bf16[176,3072]{1,0:T(8,128)(2,1)}, u32[]{:S(2)}, u32[]{:S(2)}) collective-permute-start(bf16[176,3072]{1,0:T(8,128)(2,1)} %get-tuple-element.97), channel_id=1, source_target_pairs={{0,1},{1,0},{2,3},{3,2},{4,5},{5,4},{6,7},{7,6}} | collective-permute-start | bytes 3244040 | tf_op jit(solution)/shard_map/ppermute | solution.py:297
  147.6 3.4 %copy-start.2 = (f32[176,3072]{1,0:T(8,128)S(1)}, f32[176,3072]{1,0:T(8,128)}, u32[]{:S(2)}) copy-start(f32[176,3072]{1,0:T(8,128)} %get-tuple-element.96) | copy-start | bytes 6488068
  147.6 6.4 %collective-permute-start.14 = (bf16[176,3072]{1,0:T(8,128)(2,1)}, bf16[176,3072]{1,0:T(8,128)(2,1)}, u32[]{:S(2)}, u32[]{:S(2)}) collective-permute-start(bf16[176,3072]{1,0:T(8,128)(2,1)} %collective-permute-done.13.refs_4_), channel_id=1, source_target_pairs={{0,1},{1,0},{2,3},{3,2},{4,5},{5,4},{6,7},{7,6}} | collective-permute-start | bytes 3244040 | tf_op jit(solution)/shard_map/ppermute | solution.py:297
  150.4 50.7 %collective-permute-start.6 = (bf16[176,3072]{1,0:T(8,128)(2,1)}, bf16[176,3072]{1,0:T(8,128)(2,1)S(1)}, u32[]{:S(2)}, u32[]{:S(2)}) collective-permute-start(bf16[176,3072]{1,0:T(8,128)(2,1)} %add_convert_fusion.1), channel_id=1, source_target_pairs={{0,2},{1,3},{2,0},{3,1},{4,6},{5,7},{6,4},{7,5}} | collective-permute-start | bytes 3244040 | tf_op jit(solution)/shard_map/ppermute | solution.py:298
  152.5 48.6 %collective-permute-start.10 = (bf16[176,3072]{1,0:T(8,128)(2,1)S(1)}, bf16[176,3072]{1,0:T(8,128)(2,1)S(1)}, u32[]{:S(2)}, u32[]{:S(2)}) collective-permute-start(bf16[176,3072]{1,0:T(8,128)(2,1)S(1)} %add_convert_fusion), channel_id=1, source_target_pairs={{0,2},{1,3},{2,0},{3,1},{4,6},{5,7},{6,4},{7,5}} | collective-permute-start | bytes 3244040 | tf_op jit(solution)/shard_map/ppermute | solution.py:298
  201.1 2.2 %copy-start = (f32[352,3072]{1,0:T(8,128)S(1)}, f32[352,3072]{1,0:T(8,128)}, u32[]{:S(2)}) copy-start(f32[352,3072]{1,0:T(8,128)} %convert_add_fusion.chip) | copy-start | bytes 12976132
